TPU v7x, 128 devices: a whole 4x4x4 slice. The times are simulated.
128 devices in a mesh: scen: 8 (over x_hi, y), slab: 16 (over z, x_lo, core).
Axes of the slice: x: 4 (x_hi: 2, x_lo: 2; x = x_hi * 2 + x_lo), y: 4, z: 4, core: 2. Of those that a mesh axis runs over, the one named last changes fastest.
Arguments:
- start: float32 [8, 128, 256, 256], P('scen', 'slab'), may hold values from 0 to 2
- flow_east: float32 [8, 128, 256, 256], P('scen', 'slab'), may hold values from 0.3 to 1.2
- flow_north: float32 [8, 128, 256, 256], P('scen', 'slab'), may hold values from 0.3 to 1.2
- wells: int32 [128, 256, 256], P('slab'), may hold values 0 or 1
- monitors: int32 [128, 256, 256], P('slab'), may hold values 0 or 1
- control: float32 [8, 32, 4096], P('scen', 'slab'), may hold values from -3 to 3
- multiplier: float32 [8, 32, 4096], P('scen', 'slab'), may hold values from -3 to 3
- threshold: float32 [1], replicated, may hold values from 0.8 to 1.3
Outputs:
- final_fields: float32 [8, 128, 256, 256], P('scen', 'slab')
- consensus_next: float32 [32, 4096], P('slab')
- multiplier_next: float32 [8, 32, 4096], P('scen', 'slab')
- cvar: float32 [1], replicated
All inputs are finite; a program needn't handle non-finite values. No bound on the sum of `wells` or of `monitors` on one device may be relied on, other than what follows from the above.
Results may differ from a plain program's by a relative error of at most 0.00002.
Values sent between devices are 32-bit elements; how exact they have to be, the bound alone decides.
No kernel may reach another device: no remote copies, remote signals or barrier semaphores. Data moves between devices by JAX's collectives and lax.ppermute only.
A program may use at most 192 MiB of HBM per device.

v0:
```python
import jax
import jax.numpy as jnp
from jax import lax
from jax.sharding import PartitionSpec as P

STEPS = 4
EPS_LIMIT = 0.01
TIME_STEP = 0.25
DIFF_FLAT = 0.1
DIFF_VERTICAL = 0.25
BETA_LEVEL = 0.75
SOFT_WIDTH = 0.25


def with_halo(cells, sides, width):
    for axis, dim in sides:
        count = lax.axis_size(axis)
        ends = count - 1
        head = lax.slice_in_dim(cells, 0, width, axis=dim)
        tail = lax.slice_in_dim(cells, cells.shape[dim] - width, cells.shape[dim], axis=dim)
        cells = jnp.concatenate(
            [
                lax.ppermute(tail, axis, [(i, (i + 1) % count) for i in range(ends)]),
                cells,
                lax.ppermute(head, axis, [((i + 1) % count, i) for i in range(ends)]),
            ],
            axis=dim,
        )
    return cells


def pad_axis(field, which_axis, low_pad, high_pad):
    widths = [(0, 0)] * field.ndim
    widths[which_axis] = (low_pad, high_pad)
    return jnp.pad(field, widths)


def second_difference(padded, field, which_axis):
    length = field.shape[which_axis]
    upper_cells = lax.slice_in_dim(padded, 2, length + 2, axis=which_axis)
    lower_cells = lax.slice_in_dim(padded, 0, length, axis=which_axis)
    return upper_cells - 2.0 * field + lower_cells


def divergence(field, velocity, which_axis):
    length = field.shape[which_axis]
    padded = pad_axis(field, which_axis, 1, 1)
    lower_cells = lax.slice_in_dim(padded, 0, length, axis=which_axis)
    upper_cells = lax.slice_in_dim(padded, 2, length + 2, axis=which_axis)
    backward = field - lower_cells
    forward = upper_cells - field
    product = backward * forward
    weight = (product + jnp.sqrt(product * product + EPS_LIMIT * EPS_LIMIT)) / (
        backward * backward + forward * forward + EPS_LIMIT
    )
    face_value = field + 0.5 * weight * (backward / 3.0 + 2.0 * forward / 3.0)
    fluxes = velocity * face_value
    previous = lax.slice_in_dim(pad_axis(fluxes, which_axis, 1, 0), 0, length, axis=which_axis)
    return fluxes - previous


def horizontal(field, flow_east, flow_north, rate):
    advect = divergence(field, flow_east, 1) + divergence(field, flow_north, 2)
    spread = second_difference(pad_axis(field, 1, 1, 1), field, 1) + second_difference(
        pad_axis(field, 2, 1, 1), field, 2
    )
    return -advect + DIFF_FLAT * spread - rate * field


def prolong(coarse, row_count, column_count):
    plane_count = coarse.shape[0]
    cube = coarse.reshape(plane_count, 1, row_count // 4, 1, column_count // 4, 1)
    cube = jnp.broadcast_to(cube, (plane_count, 4, row_count // 4, 4, column_count // 4, 4))
    return cube.reshape(plane_count * 4, row_count, column_count)


def restrict(fine):
    plane_count, row_count, column_count = fine.shape
    blocks = fine.reshape(plane_count // 4, 4, row_count // 4, 4, column_count // 4, 4).sum(
        axis=(1, 3, 5)
    )
    return blocks.reshape(plane_count // 4, row_count // 4 * (column_count // 4))


def on_device(start, flow_east, flow_north, wells, monitors, control, multiplier, threshold):
    scen_count = lax.axis_size("scen")
    slab_count = lax.axis_size("slab")
    consensus = lax.psum(jnp.sum(control + multiplier, axis=0), "scen") / scen_count
    field = start[0]
    east = flow_east[0]
    north = flow_north[0]
    plane_count, row_count, column_count = field.shape
    wells_float = wells.astype(jnp.float32)
    monitor_float = monitors.astype(jnp.float32)
    rate = wells_float * prolong(consensus, row_count, column_count)
    states = []
    for step_index in range(STEPS):
        states.append(field)
        padded = with_halo(field, (("slab", 0),), 1)
        vertical = second_difference(padded, field, 0)
        field = field + TIME_STEP * (
            horizontal(field, east, north, rate) + DIFF_VERTICAL * vertical
        )
    mass, count = lax.psum((jnp.sum(monitor_float * field * field), jnp.sum(monitor_float)), "slab")
    count = jnp.maximum(count, 1.0)
    loss = mass / count
    scaled = (loss - threshold[0]) / SOFT_WIDTH
    weight = jax.nn.sigmoid(scaled) / ((1.0 - BETA_LEVEL) * scen_count)
    soft_term = SOFT_WIDTH * jax.nn.softplus(scaled) / ((1.0 - BETA_LEVEL) * scen_count)
    risk = lax.psum(soft_term, "scen")
    adjoint = weight * 2.0 * monitor_float * field / count
    rate_grad = jnp.zeros_like(field)
    for step_index in reversed(range(STEPS)):
        state = states[step_index]
        padded = with_halo(adjoint, (("slab", 0),), 1)
        unused, pullback = jax.vjp(lambda values: horizontal(values, east, north, rate), state)
        (pulled,) = pullback(adjoint)
        rate_grad = rate_grad - TIME_STEP * state * adjoint
        vertical = second_difference(padded, adjoint, 0)
        adjoint = adjoint + TIME_STEP * (pulled + DIFF_VERTICAL * vertical)
    coarse_cells = plane_count * slab_count * row_count * column_count / 64.0
    gradient = coarse_cells * restrict(wells_float * rate_grad)
    total = lax.psum(gradient, "scen")
    consensus_next = consensus - total
    multiplier_next = multiplier + control - consensus_next[None]
    cvar = threshold + risk
    return (field[None], consensus_next, multiplier_next, cvar)


def solution(mesh):
    placed = (
        P("scen", "slab", None, None),
        P("scen", "slab", None, None),
        P("scen", "slab", None, None),
        P("slab", None, None),
        P("slab", None, None),
        P("scen", "slab", None),
        P("scen", "slab", None),
        P(),
    )
    return jax.shard_map(
        on_device,
        mesh=mesh,
        in_specs=placed,
        out_specs=(P("scen", "slab", None, None), P("slab", None), P("scen", "slab", None), P()),
        check_vma=False,
    )
```

profile of v0, /device:TPU:2, one launch (start us, length us, event | category | flops | bytes accessed | tf_op | source)
XLA Modules:
  0.0 485.9 jit_solution(5351484315725654341)
XLA Ops:
  0.6 1.1 slice_bitcast_fusion.1
  1.7 1.9 collective-permute-start
  3.6 2.4 collective-permute-start.1
  6.0 0.8 add.433
  6.9 41.1 %psum.35 = f32[2,4096]{1,0:T(2,128)S(1)} all-reduce(f32[2,4096]{1,0:T(2,128)S(1)} %bitcast.40), channel_id=1, replica_groups=mesh['scen'=8,'slab'=16] {'scen'}, use_global_device_ids=true, to_apply=%region_0.0 | all-reduce | flops 8192 | bytes 65536 | tf_op jit(solution)/shard_map/psum | solution.py:88
  48.0 11.3 %bitcast_multiply_fusion.3 = (f32[8,256,256]{2,1,0:T(8,128)}, f32[8,256,256]{2,1,0:T(8,128)}) fusion(f32[1,8,256,256]{3,2,1,0:T(8,128)} %param.10, f32[8,256,256]{2,1,0:T(8,128)} %bitcast.37, f32[1,8,256,256]{3,2,1,0:T(8,128)} %param.9), kind=kLoop, calls=%fused_computation.197 | loop fusion | flops 18874368 | bytes 10485760 | tf_op jit(solution)/shard_map/mul | solution.py:57
  59.3 0.1 broadcast_in_dim.16
  59.4 21.5 %broadcast_in_dim.17 = f32[2,4,64,4,64,4]{5,4,3,2,1,0:T(8,128)} broadcast(f32[2,64,64]{2,1,0:T(8,128)S(1)} %broadcast_in_dim.16), dimensions={0,2,4} | broadcast | bytes 2129920 | tf_op jit(solution)/shard_map/broadcast_in_dim | solution.py:73
  80.9 56.1 %reshape.22 = f32[8,256,256]{2,1,0:T(8,128)} reshape(f32[2,4,64,4,64,4]{5,4,3,2,1,0:T(8,128)} %broadcast_in_dim.17) | data formatting | bytes 4194304 | tf_op jit(solution)/shard_map/reshape | solution.py:74
  137.6 0.0 copy-start
  137.7 12.0 %fusion.7 = (f32[8,256,256]{2,1,0:T(8,128)S(1)}, f32[8,256,256]{2,1,0:T(8,128)S(1)}) fusion(f32[8,256,256]{2,1,0:T(8,128)} %bitcast.38, f32[8,256,256]{2,1,0:T(8,128)} %get-tuple-element.78, f32[8,256,256]{2,1,0:T(8,128)} %get-tuple-element.77, f32[1,256,256]{2,1,0:T(8,128)S(1)} %collective-permute-done.1, f32[1,256,256]{2,1,0:T(8,128)S(1)} %collective-permute-done, ...), kind=kLoop, calls=%fused_computation.48 | loop fusion | flops 12582912 | bytes 15204352 | tf_op jit(solution)/shard_map/add | solution.py:101
  149.7 1.9 collective-permute-start.2
  151.7 2.4 collective-permute-start.3
  154.1 4.1 bitcast_multiply_fusion.2
  158.3 1.1 collective-permute-done.3
  159.4 3.2 fusion.15
  162.6 2.1 collective-permute-start.4
  164.7 3.4 collective-permute-start.5
  168.0 4.1 bitcast_multiply_fusion.1
  172.2 0.2 collective-permute-done.5
  172.4 3.0 fusion.23
  175.5 2.4 collective-permute-start.6
  177.9 4.1 collective-permute-start.7
  182.0 4.1 bitcast_multiply_fusion.4
  186.2 5.0 %fusion.42 = (f32[]{:T(128)}, f32[]{:T(128)}, f32[8,256,256]{2,1,0:T(8,128)}) fusion(s32[8,256,256]{2,1,0:T(8,128)S(1)} %copy-done.21, f32[8,256,256]{2,1,0:T(8,128)S(1)} %fusion.23, f32[1,256,256]{2,1,0:T(8,128)S(1)} %collective-permute-done.7, f32[1,256,256]{2,1,0:T(8,128)S(1)} %collective-permute-done.6, f32[8,256,256]{2,1,0:T(8,128)S(1)} %get-tuple-element.44, ...), kind=kLoop, calls=%fused_computation.83 | loop fusion | flops 14155774 | bytes 13107208 | tf_op jit(solution)/shard_map/reduce_sum | solution.py:104
  191.2 27.7 %all-reduce.46 = (f32[]{:T(128)}, f32[]{:T(128)}) all-reduce(f32[]{:T(128)} %get-tuple-element.5, f32[]{:T(128)} %get-tuple-element.4), channel_id=1, replica_groups=mesh['scen'=8,'slab'=16] {'slab'}, use_global_device_ids=true, to_apply=%region_4.5 | all-reduce | flops 2 | bytes 16 | tf_op jit(solution)/shard_map/psum | solution.py:104
  220.2 4.4 broadcast_multiply_fusion.2
  224.6 8.3 %fusion.45 = (f32[8,256,256]{2,1,0:T(8,128)}, f32[8,256,256]{2,1,0:T(8,128)S(1)}, f32[8,256,256]{2,1,0:T(8,128)}, f32[8,256,256]{2,1,0:T(8,128)S(1)}) fusion(f32[8,256,256]{2,1,0:T(8,128)S(1)} %copy-done.10, f32[8,256,256]{2,1,0:T(8,128)S(1)} %get-tuple-element.33, f32[1,8,256,256]{3,2,1,0:T(8,128)S(1)} %copy-done, f32[1,8,256,256]{3,2,1,0:T(8,128)S(1)} %copy-done.2), kind=kLoop, calls=%fused_computation.86 | loop fusion | flops 39321600 | bytes 16777216 | tf_op jit(solution)/shard_map/transpose(jvp())/add_any | solution.py:52
  232.9 5.3 %collective-permute-start.8 = (f32[1,256,256]{2,1,0:T(8,128)S(1)}, f32[1,256,256]{2,1,0:T(8,128)S(1)}, u32[]{:S(2)}, u32[]{:S(2)}) collective-permute-start(f32[1,256,256]{2,1,0:T(8,128)S(1)} %get-tuple-element.61), channel_id=1, source_target_pairs={{1,0},{2,1},{3,2},{4,3},{5,4},{6,5},{7,6},{8,7},{9,8},{10,9},{11,1... | collective-permute-start | bytes 786440 | tf_op jit(solution)/shard_map/ppermute | solution.py:25
  238.2 2.4 collective-permute-start.9
  240.7 8.5 %fusion.190 = (f32[8,256,256]{2,1,0:T(8,128)}, f32[8,256,256]{2,1,0:T(8,128)}, f32[8,256,256]{2,1,0:T(8,128)}, f32[8,256,256]{2,1,0:T(8,128)}) fusion(f32[8,256,256]{2,1,0:T(8,128)S(1)} %get-tuple-element.35, f32[8,256,256]{2,1,0:T(8,128)S(1)} %copy-done.10, f32[8,256,256]{2,1,0:T(8,128)S(1)} %get-tuple-element.50), kind=kLoop, calls=%fused_computation.312 | loop fusion | flops 37748736 | bytes 14680064 | tf_op jit(solution)/shard_map/transpose(jvp())/neg | solution.py:50
  249.4 16.8 %broadcast_multiply_fusion.1 = (f32[8,256,256]{2,1,0:T(8,128)}, f32[8,256,256]{2,1,0:T(8,128)S(1)}) fusion(f32[8,256,256]{2,1,0:T(8,128)} %copy-done.13, f32[1,256,256]{2,1,0:T(8,128)S(1)} %collective-permute-done.9, f32[1,256,256]{2,1,0:T(8,128)S(1)} %collective-permute-done.8, f32[8,256,256]{2,1,0:T(8,128)} %get-tuple-element.59, ...), kind=kLoop, calls=%fused_computation.294 | loop fusion | flops 16777216 | bytes 27787264 | tf_op jit(solution)/shard_map/transpose(jvp())/mul | solution.py:67
  266.2 8.3 %fusion.51 = (f32[8,256,256]{2,1,0:T(8,128)}, f32[8,256,256]{2,1,0:T(8,128)S(1)}, f32[8,256,256]{2,1,0:T(8,128)}, f32[8,256,256]{2,1,0:T(8,128)S(1)}) fusion(f32[8,256,256]{2,1,0:T(8,128)S(1)} %copy-done.8, f32[8,256,256]{2,1,0:T(8,128)S(1)} %get-tuple-element.23, f32[1,8,256,256]{3,2,1,0:T(8,128)S(1)} %copy-done, f32[1,8,256,256]{3,2,1,0:T(8,128)S(1)} %copy-done.3), kind=kLoop, calls=%fused_computation.92 | loop fusion | flops 39321600 | bytes 16777216 | tf_op jit(solution)/shard_map/transpose(jvp())/add_any | solution.py:52
  274.5 3.6 collective-permute-start.10
  278.2 2.1 collective-permute-start.11
  280.3 8.4 %fusion.184 = (f32[8,256,256]{2,1,0:T(8,128)}, f32[8,256,256]{2,1,0:T(8,128)}, f32[8,256,256]{2,1,0:T(8,128)}, f32[8,256,256]{2,1,0:T(8,128)}) fusion(f32[8,256,256]{2,1,0:T(8,128)S(1)} %get-tuple-element.25, f32[8,256,256]{2,1,0:T(8,128)S(1)} %copy-done.8, f32[8,256,256]{2,1,0:T(8,128)S(1)} %get-tuple-element.48), kind=kLoop, calls=%fused_computation.310 | loop fusion | flops 37748736 | bytes 14680064 | tf_op jit(solution)/shard_map/transpose(jvp())/neg | solution.py:50
  288.8 16.4 %broadcast_multiply_fusion = (f32[8,256,256]{2,1,0:T(8,128)}, f32[8,256,256]{2,1,0:T(8,128)}) fusion(f32[8,256,256]{2,1,0:T(8,128)} %copy-done.14, f32[1,256,256]{2,1,0:T(8,128)S(1)} %collective-permute-done.11, f32[1,256,256]{2,1,0:T(8,128)S(1)} %collective-permute-done.10, f32[8,256,256]{2,1,0:T(8,128)} %get-tuple-element.55, ...), kind=kLoop, calls=%fused_computation.293 | loop fusion | flops 16777216 | bytes 27787264 | tf_op jit(solution)/shard_map/transpose(jvp())/mul | solution.py:67
  305.2 10.2 %fusion.57 = (f32[8,256,256]{2,1,0:T(8,128)}, f32[8,256,256]{2,1,0:T(8,128)S(1)}, f32[8,256,256]{2,1,0:T(8,128)}, f32[8,256,256]{2,1,0:T(8,128)S(1)}) fusion(f32[8,256,256]{2,1,0:T(8,128)S(1)} %copy-done.12, f32[8,256,256]{2,1,0:T(8,128)} %get-tuple-element.13, f32[1,8,256,256]{3,2,1,0:T(8,128)S(1)} %copy-done, f32[1,8,256,256]{3,2,1,0:T(8,128)S(1)} %copy-done.3), kind=kLoop, calls=%fused_computation.98 | loop fusion | flops 39321600 | bytes 16777216 | tf_op jit(solution)/shard_map/transpose(jvp())/add_any | solution.py:52
  315.4 1.4 fusion.196
  316.8 3.6 collective-permute-start.12
  320.5 2.1 collective-permute-start.13
  322.6 8.5 %fusion.177 = (f32[8,256,256]{2,1,0:T(8,128)}, f32[8,256,256]{2,1,0:T(8,128)}, f32[8,256,256]{2,1,0:T(8,128)}, f32[8,256,256]{2,1,0:T(8,128)}) fusion(f32[8,256,256]{2,1,0:T(8,128)S(1)} %get-tuple-element.15, f32[8,256,256]{2,1,0:T(8,128)S(1)} %copy-done.12, f32[8,256,256]{2,1,0:T(8,128)S(1)} %get-tuple-element.46), kind=kLoop, calls=%fused_computation.308 | loop fusion | flops 37748736 | bytes 14680064 | tf_op jit(solution)/shard_map/transpose(jvp())/neg | solution.py:50
  331.1 21.2 %fusion.68 = f32[8,256,256]{2,1,0:T(8,128)} fusion(f32[8,256,256]{2,1,0:T(8,128)} %get-tuple-element.13, f32[1,256,256]{2,1,0:T(8,128)S(1)} %collective-permute-done.13, f32[1,256,256]{2,1,0:T(8,128)S(1)} %collective-permute-done.12, f32[8,256,256]{2,1,0:T(8,128)} %get-tuple-element.51, f32[8,256,256]{2,1,0:T(8,128)} %get-tuple-element.45, ...), kind=kLoop, calls=%fused_computation.110 | loop fusion | flops 23592960 | bytes 40370176 | tf_op jit(solution)/shard_map/mul | solution.py:122
  352.4 71.4 %reshape.23 = f32[2,4,64,4,64,4]{5,4,3,2,1,0:T(8,128)} reshape(f32[8,256,256]{2,1,0:T(8,128)} %fusion.68) | data formatting | bytes 4194304 | tf_op jit(solution)/shard_map/reshape | solution.py:79
  423.8 20.8 %reduce_sum.36 = f32[2,64,64]{2,1,0:T(8,128)S(1)} reduce(f32[2,4,64,4,64,4]{5,4,3,2,1,0:T(8,128)} %reshape.23, f32[]{:T(128)} %constant.83.clone.1), dimensions={1,3,5}, to_apply=%region_5.6 | reduce | flops 516096 | bytes 2129924 | tf_op jit(solution)/shard_map/reduce_sum | solution.py:79
  444.6 0.1 mul.858
  444.7 38.5 %all-reduce.47 = (f32[2,4096]{1,0:T(2,128)S(1)}, f32[1]{0:T(128)}) all-reduce(f32[2,4096]{1,0:T(2,128)S(1)} %mul.858, f32[1]{0:T(128)} %bitcast.9), channel_id=1, replica_groups=mesh['scen'=8,'slab'=16] {'scen'}, use_global_device_ids=true, to_apply=%region_6.7 | all-reduce | flops 8193 | bytes 65544 | tf_op jit(solution)/shard_map/psum | solution.py:123
  483.2 0.7 bitcast_subtract_fusion
  (70 shorter events, 0.3 us)
Async XLA Ops:
  1.7 135.9 %collective-permute-start = (f32[1,256,256]{2,1,0:T(8,128)S(1)}, f32[1,256,256]{2,1,0:T(8,128)S(1)}, u32[]{:S(2)}, u32[]{:S(2)}) collective-permute-start(f32[1,256,256]{2,1,0:T(8,128)S(1)} %get-tuple-element.75), channel_id=1, source_target_pairs={{1,0},{2,1},{3,2},{4,3},{5,4},{6,5},{7,6},{8,7},{9,8},{10,9},{11,1... | collective-permute-start | bytes 786440 | tf_op jit(solution)/shard_map/ppermute | solution.py:25
  3.6 134.0 %collective-permute-start.1 = (f32[1,256,256]{2,1,0:T(8,128)S(1)}, f32[1,256,256]{2,1,0:T(8,128)S(1)}, u32[]{:S(2)}, u32[]{:S(2)}) collective-permute-start(f32[1,256,256]{2,1,0:T(8,128)S(1)} %get-tuple-element.76), channel_id=1, source_target_pairs={{0,1},{1,2},{2,3},{3,4},{4,5},{5,6},{6,7},{7,8},{8,9},{9,10},{10,1... | collective-permute-start | bytes 786440 | tf_op jit(solution)/shard_map/ppermute | solution.py:23
  6.8 52.4 %copy-start.22 = (f32[1,2,4096]{2,1,0:T(2,128)}, f32[1,2,4096]{2,1,0:T(2,128)S(1)}, u32[]{:S(2)}) copy-start(f32[1,2,4096]{2,1,0:T(2,128)S(1)} %add.433) | copy-start | bytes 98308
  47.9 11.3 %copy-start.24 = (f32[2,4096]{1,0:T(2,128)}, f32[2,4096]{1,0:T(2,128)S(1)}, u32[]{:S(2)}) copy-start(f32[2,4096]{1,0:T(2,128)S(1)} %psum.35) | copy-start | bytes 98308
  137.6 16.4 %copy-start = (f32[1,8,256,256]{3,2,1,0:T(8,128)S(1)}, f32[1,8,256,256]{3,2,1,0:T(8,128)}, u32[]{:S(2)}) copy-start(f32[1,8,256,256]{3,2,1,0:T(8,128)} %param.10) | copy-start | bytes 6291460
  137.7 16.4 %copy-start.1 = (f32[1,8,256,256]{3,2,1,0:T(8,128)S(1)}, f32[1,8,256,256]{3,2,1,0:T(8,128)}, u32[]{:S(2)}) copy-start(f32[1,8,256,256]{3,2,1,0:T(8,128)} %param.9) | copy-start | bytes 6291460
  149.7 9.7 %copy-start.11 = (f32[8,256,256]{2,1,0:T(8,128)}, f32[8,256,256]{2,1,0:T(8,128)S(1)}, u32[]{:S(2)}) copy-start(f32[8,256,256]{2,1,0:T(8,128)S(1)} %get-tuple-element.43) | copy-start | bytes 6291460
  149.7 36.4 %copy-start.4 = (f32[8,256,256]{2,1,0:T(8,128)}, f32[8,256,256]{2,1,0:T(8,128)S(1)}, u32[]{:S(2)}) copy-start(f32[8,256,256]{2,1,0:T(8,128)S(1)} %get-tuple-element.44) | copy-start | bytes 6291460
  149.7 8.5 %collective-permute-start.2 = (f32[1,256,256]{2,1,0:T(8,128)S(1)}, f32[1,256,256]{2,1,0:T(8,128)S(1)}, u32[]{:S(2)}, u32[]{:S(2)}) collective-permute-start(f32[1,256,256]{2,1,0:T(8,128)S(1)} %get-tuple-element.71), channel_id=1, source_target_pairs={{1,0},{2,1},{3,2},{4,3},{5,4},{6,5},{7,6},{8,7},{9,8},{10,9},{11,1... | collective-permute-start | bytes 786440 | tf_op jit(solution)/shard_map/ppermute | solution.py:25
  151.7 7.7 %collective-permute-start.3 = (f32[1,256,256]{2,1,0:T(8,128)S(1)}, f32[1,256,256]{2,1,0:T(8,128)S(1)}, u32[]{:S(2)}, u32[]{:S(2)}) collective-permute-start(f32[1,256,256]{2,1,0:T(8,128)S(1)} %get-tuple-element.72), channel_id=1, source_target_pairs={{0,1},{1,2},{2,3},{3,4},{4,5},{5,6},{6,7},{7,8},{8,9},{9,10},{10,1... | collective-permute-start | bytes 786440 | tf_op jit(solution)/shard_map/ppermute | solution.py:23
  162.5 9.8 %copy-start.7 = (f32[8,256,256]{2,1,0:T(8,128)}, f32[8,256,256]{2,1,0:T(8,128)S(1)}, u32[]{:S(2)}) copy-start(f32[8,256,256]{2,1,0:T(8,128)S(1)} %fusion.15) | copy-start | bytes 6291460
  162.6 9.6 %collective-permute-start.4 = (f32[1,256,256]{2,1,0:T(8,128)S(1)}, f32[1,256,256]{2,1,0:T(8,128)S(1)}, u32[]{:S(2)}, u32[]{:S(2)}) collective-permute-start(f32[1,256,256]{2,1,0:T(8,128)S(1)} %get-tuple-element.67), channel_id=1, source_target_pairs={{1,0},{2,1},{3,2},{4,3},{5,4},{6,5},{7,6},{8,7},{9,8},{10,9},{11,1... | collective-permute-start | bytes 786440 | tf_op jit(solution)/shard_map/ppermute | solution.py:25
  164.7 7.7 %collective-permute-start.5 = (f32[1,256,256]{2,1,0:T(8,128)S(1)}, f32[1,256,256]{2,1,0:T(8,128)S(1)}, u32[]{:S(2)}, u32[]{:S(2)}) collective-permute-start(f32[1,256,256]{2,1,0:T(8,128)S(1)} %get-tuple-element.68), channel_id=1, source_target_pairs={{0,1},{1,2},{2,3},{3,4},{4,5},{5,6},{6,7},{7,8},{8,9},{9,10},{10,1... | collective-permute-start | bytes 786440 | tf_op jit(solution)/shard_map/ppermute | solution.py:23
  175.4 10.7 %copy-start.9 = (f32[8,256,256]{2,1,0:T(8,128)}, f32[8,256,256]{2,1,0:T(8,128)S(1)}, u32[]{:S(2)}) copy-start(f32[8,256,256]{2,1,0:T(8,128)S(1)} %fusion.23) | copy-start | bytes 6291460
  175.5 10.6 %collective-permute-start.6 = (f32[1,256,256]{2,1,0:T(8,128)S(1)}, f32[1,256,256]{2,1,0:T(8,128)S(1)}, u32[]{:S(2)}, u32[]{:S(2)}) collective-permute-start(f32[1,256,256]{2,1,0:T(8,128)S(1)} %get-tuple-element.65), channel_id=1, source_target_pairs={{1,0},{2,1},{3,2},{4,3},{5,4},{6,5},{7,6},{8,7},{9,8},{10,9},{11,1... | collective-permute-start | bytes 786440 | tf_op jit(solution)/shard_map/ppermute | solution.py:25
  177.8 8.3 %copy-start.21 = (s32[8,256,256]{2,1,0:T(8,128)S(1)}, s32[8,256,256]{2,1,0:T(8,128)}, u32[]{:S(2)}) copy-start(s32[8,256,256]{2,1,0:T(8,128)} %param.12) | copy-start | bytes 6291460
  177.9 8.3 %collective-permute-start.7 = (f32[1,256,256]{2,1,0:T(8,128)S(1)}, f32[1,256,256]{2,1,0:T(8,128)S(1)}, u32[]{:S(2)}, u32[]{:S(2)}) collective-permute-start(f32[1,256,256]{2,1,0:T(8,128)S(1)} %get-tuple-element.66), channel_id=1, source_target_pairs={{0,1},{1,2},{2,3},{3,4},{4,5},{5,6},{6,7},{7,8},{8,9},{9,10},{10,1... | collective-permute-start | bytes 786440 | tf_op jit(solution)/shard_map/ppermute | solution.py:23
  220.2 4.4 copy-start.2
  220.2 4.4 copy-start.10
  224.6 8.3 %copy-start.13 = (f32[8,256,256]{2,1,0:T(8,128)}, f32[8,256,256]{2,1,0:T(8,128)S(1)}, u32[]{:S(2)}) copy-start(f32[8,256,256]{2,1,0:T(8,128)S(1)} %get-tuple-element.33) | copy-start | bytes 6291460
  232.8 7.8 %copy-start.17 = (f32[8,256,256]{2,1,0:T(8,128)}, f32[8,256,256]{2,1,0:T(8,128)S(1)}, u32[]{:S(2)}) copy-start(f32[8,256,256]{2,1,0:T(8,128)S(1)} %get-tuple-element.35) | copy-start | bytes 6291460
  232.8 7.8 %copy-start.18 = (f32[8,256,256]{2,1,0:T(8,128)}, f32[8,256,256]{2,1,0:T(8,128)S(1)}, u32[]{:S(2)}) copy-start(f32[8,256,256]{2,1,0:T(8,128)S(1)} %get-tuple-element.50) | copy-start | bytes 6291460
  232.9 16.4 %collective-permute-start.8 = (f32[1,256,256]{2,1,0:T(8,128)S(1)}, f32[1,256,256]{2,1,0:T(8,128)S(1)}, u32[]{:S(2)}, u32[]{:S(2)}) collective-permute-start(f32[1,256,256]{2,1,0:T(8,128)S(1)} %get-tuple-element.61), channel_id=1, source_target_pairs={{1,0},{2,1},{3,2},{4,3},{5,4},{6,5},{7,6},{8,7},{9,8},{10,9},{11,1... | collective-permute-start | bytes 786440 | tf_op jit(solution)/shard_map/ppermute | solution.py:25
  238.2 11.1 %collective-permute-start.9 = (f32[1,256,256]{2,1,0:T(8,128)S(1)}, f32[1,256,256]{2,1,0:T(8,128)S(1)}, u32[]{:S(2)}, u32[]{:S(2)}) collective-permute-start(f32[1,256,256]{2,1,0:T(8,128)S(1)} %get-tuple-element.62), channel_id=1, source_target_pairs={{0,1},{1,2},{2,3},{3,4},{4,5},{5,6},{6,7},{7,8},{8,9},{9,10},{10,1... | collective-permute-start | bytes 786440 | tf_op jit(solution)/shard_map/ppermute | solution.py:23
  249.3 16.8 %copy-start.3 = (f32[1,8,256,256]{3,2,1,0:T(8,128)S(1)}, f32[1,8,256,256]{3,2,1,0:T(8,128)}, u32[]{:S(2)}) copy-start(f32[1,8,256,256]{3,2,1,0:T(8,128)} %param.9) | copy-start | bytes 6291460
  249.3 16.8 %copy-start.8 = (f32[8,256,256]{2,1,0:T(8,128)S(1)}, f32[8,256,256]{2,1,0:T(8,128)}, u32[]{:S(2)}) copy-start(f32[8,256,256]{2,1,0:T(8,128)} %copy-done.7) | copy-start | bytes 6291460
  266.1 8.3 %copy-start.14 = (f32[8,256,256]{2,1,0:T(8,128)}, f32[8,256,256]{2,1,0:T(8,128)S(1)}, u32[]{:S(2)}) copy-start(f32[8,256,256]{2,1,0:T(8,128)S(1)} %get-tuple-element.23) | copy-start | bytes 6291460
  274.5 14.3 %copy-start.19 = (f32[8,256,256]{2,1,0:T(8,128)}, f32[8,256,256]{2,1,0:T(8,128)S(1)}, u32[]{:S(2)}) copy-start(f32[8,256,256]{2,1,0:T(8,128)S(1)} %get-tuple-element.25) | copy-start | bytes 6291460
  274.5 14.3 %copy-start.20 = (f32[8,256,256]{2,1,0:T(8,128)}, f32[8,256,256]{2,1,0:T(8,128)S(1)}, u32[]{:S(2)}) copy-start(f32[8,256,256]{2,1,0:T(8,128)S(1)} %get-tuple-element.48) | copy-start | bytes 6291460
  274.5 14.2 %collective-permute-start.10 = (f32[1,256,256]{2,1,0:T(8,128)S(1)}, f32[1,256,256]{2,1,0:T(8,128)S(1)}, u32[]{:S(2)}, u32[]{:S(2)}) collective-permute-start(f32[1,256,256]{2,1,0:T(8,128)S(1)} %get-tuple-element.57), channel_id=1, source_target_pairs={{1,0},{2,1},{3,2},{4,3},{5,4},{6,5},{7,6},{8,7},{9,8},{10,9},{11,1... | collective-permute-start | bytes 786440 | tf_op jit(solution)/shard_map/ppermute | solution.py:25
  278.2 10.6 %collective-permute-start.11 = (f32[1,256,256]{2,1,0:T(8,128)S(1)}, f32[1,256,256]{2,1,0:T(8,128)S(1)}, u32[]{:S(2)}, u32[]{:S(2)}) collective-permute-start(f32[1,256,256]{2,1,0:T(8,128)S(1)} %get-tuple-element.58), channel_id=1, source_target_pairs={{0,1},{1,2},{2,3},{3,4},{4,5},{5,6},{6,7},{7,8},{8,9},{9,10},{10,1... | collective-permute-start | bytes 786440 | tf_op jit(solution)/shard_map/ppermute | solution.py:23
  280.3 8.5 %copy-start.5 = (f32[8,256,256]{2,1,0:T(8,128)S(1)}, f32[8,256,256]{2,1,0:T(8,128)}, u32[]{:S(2)}) copy-start(f32[8,256,256]{2,1,0:T(8,128)} %copy-done.4) | copy-start | bytes 6291460
  288.8 16.4 %copy-start.12 = (f32[8,256,256]{2,1,0:T(8,128)S(1)}, f32[8,256,256]{2,1,0:T(8,128)}, u32[]{:S(2)}) copy-start(f32[8,256,256]{2,1,0:T(8,128)} %copy-done.11) | copy-start | bytes 6291460
  315.4 15.8 %copy-start.15 = (f32[8,256,256]{2,1,0:T(8,128)}, f32[8,256,256]{2,1,0:T(8,128)S(1)}, u32[]{:S(2)}) copy-start(f32[8,256,256]{2,1,0:T(8,128)S(1)} %get-tuple-element.15) | copy-start | bytes 6291460
  315.4 15.8 %copy-start.16 = (f32[8,256,256]{2,1,0:T(8,128)}, f32[8,256,256]{2,1,0:T(8,128)S(1)}, u32[]{:S(2)}) copy-start(f32[8,256,256]{2,1,0:T(8,128)S(1)} %get-tuple-element.46) | copy-start | bytes 6291460
  316.8 14.3 %collective-permute-start.12 = (f32[1,256,256]{2,1,0:T(8,128)S(1)}, f32[1,256,256]{2,1,0:T(8,128)S(1)}, u32[]{:S(2)}, u32[]{:S(2)}) collective-permute-start(f32[1,256,256]{2,1,0:T(8,128)S(1)} %get-tuple-element.53), channel_id=1, source_target_pairs={{1,0},{2,1},{3,2},{4,3},{5,4},{6,5},{7,6},{8,7},{9,8},{10,9},{11,1... | collective-permute-start | bytes 786440 | tf_op jit(solution)/shard_map/ppermute | solution.py:25
  320.5 10.7 %collective-permute-start.13 = (f32[1,256,256]{2,1,0:T(8,128)S(1)}, f32[1,256,256]{2,1,0:T(8,128)S(1)}, u32[]{:S(2)}, u32[]{:S(2)}) collective-permute-start(f32[1,256,256]{2,1,0:T(8,128)S(1)} %get-tuple-element.54), channel_id=1, source_target_pairs={{0,1},{1,2},{2,3},{3,4},{4,5},{5,6},{6,7},{7,8},{8,9},{9,10},{10,1... | collective-permute-start | bytes 786440 | tf_op jit(solution)/shard_map/ppermute | solution.py:23
  322.6 8.5 %copy-start.6 = (f32[8,256,256]{2,1,0:T(8,128)S(1)}, f32[8,256,256]{2,1,0:T(8,128)}, u32[]{:S(2)}) copy-start(f32[8,256,256]{2,1,0:T(8,128)} %copy-done.4) | copy-start | bytes 6291460
  423.8 59.4 %copy-start.23 = (f32[1,2,4096]{2,1,0:T(2,128)S(1)}, f32[1,2,4096]{2,1,0:T(2,128)}, u32[]{:S(2)}) copy-start(f32[1,2,4096]{2,1,0:T(2,128)} %copy-done.22) | copy-start | bytes 98308
  423.8 59.4 %copy-start.25 = (f32[2,4096]{1,0:T(2,128)S(1)}, f32[2,4096]{1,0:T(2,128)}, u32[]{:S(2)}) copy-start(f32[2,4096]{1,0:T(2,128)} %copy-done.24) | copy-start | bytes 98308
where the time goes:
time: 494 us; the launch traced here: 486 us
  other arithmetic  180 us (36%)
  local copies, waits for them, and re-layouts  152 us (31%)
  blocking collectives  107 us (22%)
  starting transfers between devices  39.9 us (8%)
  between operations  5.33 us (1%)
    reshape x1, local copies, waits for them, and re-layouts, restrict(): fine.reshape(plane_count // 4, 4, row_count // 4, 4, column_count // 4, 4)  71.4 us
    reshape x1, local copies, waits for them, and re-layouts, prolong(): return cube.reshape(plane_count * 4, row_count, column_count)  56.1 us
    psum x1, blocking collectives, on_device(): lax.psum(jnp.sum(control + multiplier, axis=0), 'scen') / scen_count  41.1 us
    psum x1, blocking collectives, on_device(): total = lax.psum(gradient, 'scen')  38.5 us
    mul x3, other arithmetic, horizontal(): return -advect + DIFF_FLAT * spread - rate * field  37.5 us
    psum x1, blocking collectives, on_device(): lax.psum((jnp.sum(monitor_float * field * field), jnp.sum(monitor_float))...  27.7 us
    add_any x3, other arithmetic, divergence(): product = backward * forward  26.7 us
    neg x3, other arithmetic, divergence(): backward = field - lower_cells  25.5 us
  transfers between devices with their start and end apart: 14, of which 2 were waited for; matrix products, arithmetic and copies ran while one was open for 26% of the time, Pallas kernels for 0%

commit v1 on v0

--- a/solution.py
+++ b/solution.py
@@ -1,3 +1,4 @@
+import functools
 import jax
 import jax.numpy as jnp
 from jax import lax
@@ -10,6 +11,13 @@
 DIFF_VERTICAL = 0.25
 BETA_LEVEL = 0.75
 SOFT_WIDTH = 0.25
+
+
+def report_series(chunk, across):
+    return jnp.sum(lax.all_gather(chunk, across), axis=0)
+
+
+trace_quotas_for = functools.partial(report_series, across="scen")
 
 
 def with_halo(cells, sides, width):
@@ -120,7 +128,7 @@
         adjoint = adjoint + TIME_STEP * (pulled + DIFF_VERTICAL * vertical)
     coarse_cells = plane_count * slab_count * row_count * column_count / 64.0
     gradient = coarse_cells * restrict(wells_float * rate_grad)
-    total = lax.psum(gradient, "scen")
+    total = trace_quotas_for(gradient)
     consensus_next = consensus - total
     multiplier_next = multiplier + control - consensus_next[None]
     cvar = threshold + risk

time: 494 us -> 509 us (1.030)
  blocking collectives: 107 us -> 123 us
    all_gather x0 -> x1, blocking collectives: none -> 34.4 us  [report_series(): return jnp.sum(lax.all_gather(chunk, across), axis=0)]
    psum x1, blocking collectives: 38.5 us -> 20.3 us  [on_device(): risk = lax.psum(soft_term, 'scen')]
  transfers between devices with their start and end apart: 14 -> 14, of which waited for: 2 -> 1; matrix products, arithmetic and copies ran while one was open for 26% -> 26% of each run, Pallas kernels for 0% -> 0%
where the time goes in v1:
time: 509 us; the launch traced here: 500 us
  other arithmetic  180 us (35%)
  local copies, waits for them, and re-layouts  152 us (30%)
  blocking collectives  123 us (24%)
  starting transfers between devices  37.9 us (7%)
  between operations  5.38 us (1%)
    reshape x1, local copies, waits for them, and re-layouts, restrict(): fine.reshape(plane_count // 4, 4, row_count // 4, 4, column_count // 4, 4)  71.4 us
    reshape x1, local copies, waits for them, and re-layouts, prolong(): return cube.reshape(plane_count * 4, row_count, column_count)  56.1 us
    psum x1, blocking collectives, on_device(): lax.psum(jnp.sum(control + multiplier, axis=0), 'scen') / scen_count  41.1 us
    mul x3, other arithmetic, horizontal(): return -advect + DIFF_FLAT * spread - rate * field  37.5 us
    all_gather x1, blocking collectives, report_series(): return jnp.sum(lax.all_gather(chunk, across), axis=0)  34.4 us
    psum x1, blocking collectives, on_device(): lax.psum((jnp.sum(monitor_float * field * field), jnp.sum(monitor_float))...  27.5 us
    add_any x3, other arithmetic, divergence(): product = backward * forward  26.8 us
    neg x3, other arithmetic, divergence(): backward = field - lower_cells  25.6 us
  transfers between devices with their start and end apart: 14, of which 1 were waited for; matrix products, arithmetic and copies ran while one was open for 26% of the time, Pallas kernels for 0%

profile of v1, /device:TPU:2, one launch (start us, length us, event | category | flops | bytes accessed | tf_op | source)
XLA Modules:
  0.0 500.2 jit_solution(14629804327878242146)
XLA Ops:
  0.6 1.1 slice_bitcast_fusion.1
  1.7 1.9 collective-permute-start
  3.6 2.4 collective-permute-start.1
  6.0 0.8 add.431
  6.9 41.1 %psum.28 = f32[2,4096]{1,0:T(2,128)S(1)} all-reduce(f32[2,4096]{1,0:T(2,128)S(1)} %bitcast.40), channel_id=1, replica_groups=mesh['scen'=8,'slab'=16] {'scen'}, use_global_device_ids=true, to_apply=%region_0.0 | all-reduce | flops 8192 | bytes 65536 | tf_op jit(solution)/shard_map/psum | solution.py:96
  48.0 11.3 %bitcast_multiply_fusion.3 = (f32[8,256,256]{2,1,0:T(8,128)}, f32[8,256,256]{2,1,0:T(8,128)}) fusion(f32[1,8,256,256]{3,2,1,0:T(8,128)} %param.10, f32[8,256,256]{2,1,0:T(8,128)} %bitcast.37, f32[1,8,256,256]{3,2,1,0:T(8,128)} %param.9), kind=kLoop, calls=%fused_computation.197 | loop fusion | flops 18874368 | bytes 10485760 | tf_op jit(solution)/shard_map/mul | solution.py:65
  59.3 0.1 broadcast_in_dim.16
  59.4 21.5 %broadcast_in_dim.17 = f32[2,4,64,4,64,4]{5,4,3,2,1,0:T(8,128)} broadcast(f32[2,64,64]{2,1,0:T(8,128)S(1)} %broadcast_in_dim.16), dimensions={0,2,4} | broadcast | bytes 2129920 | tf_op jit(solution)/shard_map/broadcast_in_dim | solution.py:81
  81.0 56.1 %reshape.32 = f32[8,256,256]{2,1,0:T(8,128)} reshape(f32[2,4,64,4,64,4]{5,4,3,2,1,0:T(8,128)} %broadcast_in_dim.17) | data formatting | bytes 4194304 | tf_op jit(solution)/shard_map/reshape | solution.py:82
  137.7 12.0 %fusion.7 = (f32[8,256,256]{2,1,0:T(8,128)S(1)}, f32[8,256,256]{2,1,0:T(8,128)S(1)}) fusion(f32[8,256,256]{2,1,0:T(8,128)} %bitcast.38, f32[8,256,256]{2,1,0:T(8,128)} %get-tuple-element.76, f32[8,256,256]{2,1,0:T(8,128)} %get-tuple-element.75, f32[1,256,256]{2,1,0:T(8,128)S(1)} %collective-permute-done.1, f32[1,256,256]{2,1,0:T(8,128)S(1)} %collective-permute-done, ...), kind=kLoop, calls=%fused_computation.48 | loop fusion | flops 12582912 | bytes 15204352 | tf_op jit(solution)/shard_map/add | solution.py:109
  149.8 1.9 collective-permute-start.2
  151.7 2.4 collective-permute-start.3
  154.2 4.1 bitcast_multiply_fusion.2
  158.3 1.1 collective-permute-done.3
  159.4 3.2 fusion.15
  162.6 2.1 collective-permute-start.4
  164.7 3.5 collective-permute-start.5
  168.3 4.1 bitcast_multiply_fusion.1
  172.5 3.1 fusion.23
  175.6 2.5 collective-permute-start.6
  178.1 4.1 collective-permute-start.7
  182.2 4.1 bitcast_multiply_fusion.4
  186.4 5.1 %fusion.42 = (f32[]{:T(128)}, f32[]{:T(128)}, f32[8,256,256]{2,1,0:T(8,128)}) fusion(s32[8,256,256]{2,1,0:T(8,128)S(1)} %copy-done.21, f32[8,256,256]{2,1,0:T(8,128)S(1)} %fusion.23, f32[1,256,256]{2,1,0:T(8,128)S(1)} %collective-permute-done.7, f32[1,256,256]{2,1,0:T(8,128)S(1)} %collective-permute-done.6, f32[8,256,256]{2,1,0:T(8,128)S(1)} %get-tuple-element.42, ...), kind=kLoop, calls=%fused_computation.83 | loop fusion | flops 14155774 | bytes 13107208 | tf_op jit(solution)/shard_map/reduce_sum | solution.py:112
  191.5 27.5 %all-reduce.46 = (f32[]{:T(128)}, f32[]{:T(128)}) all-reduce(f32[]{:T(128)} %get-tuple-element.5, f32[]{:T(128)} %get-tuple-element.4), channel_id=1, replica_groups=mesh['scen'=8,'slab'=16] {'slab'}, use_global_device_ids=true, to_apply=%region_4.5 | all-reduce | flops 2 | bytes 16 | tf_op jit(solution)/shard_map/psum | solution.py:112
  220.3 4.3 broadcast_multiply_fusion.2
  224.7 8.3 %fusion.45 = (f32[8,256,256]{2,1,0:T(8,128)}, f32[8,256,256]{2,1,0:T(8,128)S(1)}, f32[8,256,256]{2,1,0:T(8,128)}, f32[8,256,256]{2,1,0:T(8,128)S(1)}) fusion(f32[8,256,256]{2,1,0:T(8,128)S(1)} %copy-done.10, f32[8,256,256]{2,1,0:T(8,128)S(1)} %get-tuple-element.31, f32[1,8,256,256]{3,2,1,0:T(8,128)S(1)} %copy-done, f32[1,8,256,256]{3,2,1,0:T(8,128)S(1)} %copy-done.2), kind=kLoop, calls=%fused_computation.86 | loop fusion | flops 39321600 | bytes 16777216 | tf_op jit(solution)/shard_map/transpose(jvp())/add_any | solution.py:60
  233.0 5.5 %collective-permute-start.8 = (f32[1,256,256]{2,1,0:T(8,128)S(1)}, f32[1,256,256]{2,1,0:T(8,128)S(1)}, u32[]{:S(2)}, u32[]{:S(2)}) collective-permute-start(f32[1,256,256]{2,1,0:T(8,128)S(1)} %get-tuple-element.59), channel_id=1, source_target_pairs={{1,0},{2,1},{3,2},{4,3},{5,4},{6,5},{7,6},{8,7},{9,8},{10,9},{11,1... | collective-permute-start | bytes 786440 | tf_op jit(solution)/shard_map/ppermute | solution.py:33
  238.5 1.9 collective-permute-start.9
  240.4 8.6 %fusion.190 = (f32[8,256,256]{2,1,0:T(8,128)}, f32[8,256,256]{2,1,0:T(8,128)}, f32[8,256,256]{2,1,0:T(8,128)}, f32[8,256,256]{2,1,0:T(8,128)}) fusion(f32[8,256,256]{2,1,0:T(8,128)S(1)} %get-tuple-element.33, f32[8,256,256]{2,1,0:T(8,128)S(1)} %copy-done.10, f32[8,256,256]{2,1,0:T(8,128)S(1)} %get-tuple-element.48), kind=kLoop, calls=%fused_computation.312 | loop fusion | flops 37748736 | bytes 14680064 | tf_op jit(solution)/shard_map/transpose(jvp())/neg | solution.py:58
  249.1 20.3 %psum.31 = f32[1]{0:T(128)} all-reduce(f32[1]{0:T(128)} %bitcast.9), channel_id=1, replica_groups=mesh['scen'=8,'slab'=16] {'scen'}, use_global_device_ids=true, to_apply=%region_7.8 | all-reduce | flops 1 | bytes 8 | tf_op jit(solution)/shard_map/psum | solution.py:118
  270.1 16.5 %broadcast_multiply_fusion.1 = (f32[8,256,256]{2,1,0:T(8,128)}, f32[8,256,256]{2,1,0:T(8,128)S(1)}) fusion(f32[8,256,256]{2,1,0:T(8,128)} %copy-done.13, f32[1,256,256]{2,1,0:T(8,128)S(1)} %collective-permute-done.9, f32[1,256,256]{2,1,0:T(8,128)S(1)} %collective-permute-done.8, f32[8,256,256]{2,1,0:T(8,128)} %get-tuple-element.57, ...), kind=kLoop, calls=%fused_computation.294 | loop fusion | flops 16777216 | bytes 27787264 | tf_op jit(solution)/shard_map/transpose(jvp())/mul | solution.py:75
  286.6 8.3 %fusion.51 = (f32[8,256,256]{2,1,0:T(8,128)}, f32[8,256,256]{2,1,0:T(8,128)S(1)}, f32[8,256,256]{2,1,0:T(8,128)}, f32[8,256,256]{2,1,0:T(8,128)S(1)}) fusion(f32[8,256,256]{2,1,0:T(8,128)S(1)} %copy-done.8, f32[8,256,256]{2,1,0:T(8,128)S(1)} %get-tuple-element.21, f32[1,8,256,256]{3,2,1,0:T(8,128)S(1)} %copy-done, f32[1,8,256,256]{3,2,1,0:T(8,128)S(1)} %copy-done.3), kind=kLoop, calls=%fused_computation.92 | loop fusion | flops 39321600 | bytes 16777216 | tf_op jit(solution)/shard_map/transpose(jvp())/add_any | solution.py:60
  295.0 1.9 collective-permute-start.10
  296.9 2.4 collective-permute-start.11
  299.4 8.5 %fusion.184 = (f32[8,256,256]{2,1,0:T(8,128)}, f32[8,256,256]{2,1,0:T(8,128)}, f32[8,256,256]{2,1,0:T(8,128)}, f32[8,256,256]{2,1,0:T(8,128)}) fusion(f32[8,256,256]{2,1,0:T(8,128)S(1)} %get-tuple-element.23, f32[8,256,256]{2,1,0:T(8,128)S(1)} %copy-done.8, f32[8,256,256]{2,1,0:T(8,128)S(1)} %get-tuple-element.46), kind=kLoop, calls=%fused_computation.310 | loop fusion | flops 37748736 | bytes 14680064 | tf_op jit(solution)/shard_map/transpose(jvp())/neg | solution.py:58
  307.9 16.7 %broadcast_multiply_fusion = (f32[8,256,256]{2,1,0:T(8,128)}, f32[8,256,256]{2,1,0:T(8,128)}) fusion(f32[8,256,256]{2,1,0:T(8,128)} %copy-done.14, f32[1,256,256]{2,1,0:T(8,128)S(1)} %collective-permute-done.11, f32[1,256,256]{2,1,0:T(8,128)S(1)} %collective-permute-done.10, f32[8,256,256]{2,1,0:T(8,128)} %get-tuple-element.53, ...), kind=kLoop, calls=%fused_computation.293 | loop fusion | flops 16777216 | bytes 27787264 | tf_op jit(solution)/shard_map/transpose(jvp())/mul | solution.py:75
  324.5 10.3 %fusion.57 = (f32[8,256,256]{2,1,0:T(8,128)}, f32[8,256,256]{2,1,0:T(8,128)S(1)}, f32[8,256,256]{2,1,0:T(8,128)}, f32[8,256,256]{2,1,0:T(8,128)S(1)}) fusion(f32[8,256,256]{2,1,0:T(8,128)S(1)} %copy-done.12, f32[8,256,256]{2,1,0:T(8,128)} %get-tuple-element.11, f32[1,8,256,256]{3,2,1,0:T(8,128)S(1)} %copy-done, f32[1,8,256,256]{3,2,1,0:T(8,128)S(1)} %copy-done.3), kind=kLoop, calls=%fused_computation.98 | loop fusion | flops 39321600 | bytes 16777216 | tf_op jit(solution)/shard_map/transpose(jvp())/add_any | solution.py:60
  334.8 1.4 fusion.196
  336.2 3.2 collective-permute-start.12
  339.4 2.1 collective-permute-start.13
  341.6 8.5 %fusion.177 = (f32[8,256,256]{2,1,0:T(8,128)}, f32[8,256,256]{2,1,0:T(8,128)}, f32[8,256,256]{2,1,0:T(8,128)}, f32[8,256,256]{2,1,0:T(8,128)}) fusion(f32[8,256,256]{2,1,0:T(8,128)S(1)} %get-tuple-element.13, f32[8,256,256]{2,1,0:T(8,128)S(1)} %copy-done.12, f32[8,256,256]{2,1,0:T(8,128)S(1)} %get-tuple-element.44), kind=kLoop, calls=%fused_computation.308 | loop fusion | flops 37748736 | bytes 14680064 | tf_op jit(solution)/shard_map/transpose(jvp())/neg | solution.py:58
  350.1 21.2 %fusion.68 = f32[8,256,256]{2,1,0:T(8,128)} fusion(f32[8,256,256]{2,1,0:T(8,128)} %get-tuple-element.11, f32[1,256,256]{2,1,0:T(8,128)S(1)} %collective-permute-done.13, f32[1,256,256]{2,1,0:T(8,128)S(1)} %collective-permute-done.12, f32[8,256,256]{2,1,0:T(8,128)} %get-tuple-element.49, f32[8,256,256]{2,1,0:T(8,128)} %get-tuple-element.43, ...), kind=kLoop, calls=%fused_computation.110 | loop fusion | flops 23592960 | bytes 40370176 | tf_op jit(solution)/shard_map/mul | solution.py:130
  371.3 71.4 %reshape.33 = f32[2,4,64,4,64,4]{5,4,3,2,1,0:T(8,128)} reshape(f32[8,256,256]{2,1,0:T(8,128)} %fusion.68) | data formatting | bytes 4194304 | tf_op jit(solution)/shard_map/reshape | solution.py:87
  442.8 20.8 %reduce_sum.45 = f32[2,64,64]{2,1,0:T(8,128)S(1)} reduce(f32[2,4,64,4,64,4]{5,4,3,2,1,0:T(8,128)} %reshape.33, f32[]{:T(128)} %constant.83.clone.1), dimensions={1,3,5}, to_apply=%region_5.6 | reduce | flops 516096 | bytes 2129924 | tf_op jit(solution)/shard_map/reduce_sum | solution.py:87
  463.6 0.1 mul.865
  463.7 34.4 %all_gather.4 = f32[8,2,4096]{2,1,0:T(2,128)S(1)} all-gather(f32[1,2,4096]{2,1,0:T(2,128)S(1)} %mul.865), channel_id=1, replica_groups=mesh['scen'=8,'slab'=16] {'scen'}, dimensions={0}, use_global_device_ids=true | all-gather | bytes 294912 | tf_op jit(solution)/shard_map/all_gather | solution.py:17
  498.1 0.1 reduce_sum.46
  498.2 0.7 bitcast_subtract_fusion
  (72 shorter events, 0.4 us)
Async XLA Ops:
  1.7 136.0 %collective-permute-start = (f32[1,256,256]{2,1,0:T(8,128)S(1)}, f32[1,256,256]{2,1,0:T(8,128)S(1)}, u32[]{:S(2)}, u32[]{:S(2)}) collective-permute-start(f32[1,256,256]{2,1,0:T(8,128)S(1)} %get-tuple-element.73), channel_id=1, source_target_pairs={{1,0},{2,1},{3,2},{4,3},{5,4},{6,5},{7,6},{8,7},{9,8},{10,9},{11,1... | collective-permute-start | bytes 786440 | tf_op jit(solution)/shard_map/ppermute | solution.py:33
  3.6 134.1 %collective-permute-start.1 = (f32[1,256,256]{2,1,0:T(8,128)S(1)}, f32[1,256,256]{2,1,0:T(8,128)S(1)}, u32[]{:S(2)}, u32[]{:S(2)}) collective-permute-start(f32[1,256,256]{2,1,0:T(8,128)S(1)} %get-tuple-element.74), channel_id=1, source_target_pairs={{0,1},{1,2},{2,3},{3,4},{4,5},{5,6},{6,7},{7,8},{8,9},{9,10},{10,1... | collective-permute-start | bytes 786440 | tf_op jit(solution)/shard_map/ppermute | solution.py:31
  6.8 52.4 %copy-start.22 = (f32[1,2,4096]{2,1,0:T(2,128)}, f32[1,2,4096]{2,1,0:T(2,128)S(1)}, u32[]{:S(2)}) copy-start(f32[1,2,4096]{2,1,0:T(2,128)S(1)} %add.431) | copy-start | bytes 98308
  47.9 11.3 %copy-start.24 = (f32[2,4096]{1,0:T(2,128)}, f32[2,4096]{1,0:T(2,128)S(1)}, u32[]{:S(2)}) copy-start(f32[2,4096]{1,0:T(2,128)S(1)} %psum.28) | copy-start | bytes 98308
  137.7 16.5 %copy-start = (f32[1,8,256,256]{3,2,1,0:T(8,128)S(1)}, f32[1,8,256,256]{3,2,1,0:T(8,128)}, u32[]{:S(2)}) copy-start(f32[1,8,256,256]{3,2,1,0:T(8,128)} %param.10) | copy-start | bytes 6291460
  137.7 16.5 %copy-start.1 = (f32[1,8,256,256]{3,2,1,0:T(8,128)S(1)}, f32[1,8,256,256]{3,2,1,0:T(8,128)}, u32[]{:S(2)}) copy-start(f32[1,8,256,256]{3,2,1,0:T(8,128)} %param.9) | copy-start | bytes 6291460
  149.7 9.7 %copy-start.11 = (f32[8,256,256]{2,1,0:T(8,128)}, f32[8,256,256]{2,1,0:T(8,128)S(1)}, u32[]{:S(2)}) copy-start(f32[8,256,256]{2,1,0:T(8,128)S(1)} %get-tuple-element.41) | copy-start | bytes 6291460
  149.7 36.6 %copy-start.4 = (f32[8,256,256]{2,1,0:T(8,128)}, f32[8,256,256]{2,1,0:T(8,128)S(1)}, u32[]{:S(2)}) copy-start(f32[8,256,256]{2,1,0:T(8,128)S(1)} %get-tuple-element.42) | copy-start | bytes 6291460
  149.8 8.5 %collective-permute-start.2 = (f32[1,256,256]{2,1,0:T(8,128)S(1)}, f32[1,256,256]{2,1,0:T(8,128)S(1)}, u32[]{:S(2)}, u32[]{:S(2)}) collective-permute-start(f32[1,256,256]{2,1,0:T(8,128)S(1)} %get-tuple-element.69), channel_id=1, source_target_pairs={{1,0},{2,1},{3,2},{4,3},{5,4},{6,5},{7,6},{8,7},{9,8},{10,9},{11,1... | collective-permute-start | bytes 786440 | tf_op jit(solution)/shard_map/ppermute | solution.py:33
  151.7 7.7 %collective-permute-start.3 = (f32[1,256,256]{2,1,0:T(8,128)S(1)}, f32[1,256,256]{2,1,0:T(8,128)S(1)}, u32[]{:S(2)}, u32[]{:S(2)}) collective-permute-start(f32[1,256,256]{2,1,0:T(8,128)S(1)} %get-tuple-element.70), channel_id=1, source_target_pairs={{0,1},{1,2},{2,3},{3,4},{4,5},{5,6},{6,7},{7,8},{8,9},{9,10},{10,1... | collective-permute-start | bytes 786440 | tf_op jit(solution)/shard_map/ppermute | solution.py:31
  162.6 9.9 %copy-start.7 = (f32[8,256,256]{2,1,0:T(8,128)}, f32[8,256,256]{2,1,0:T(8,128)S(1)}, u32[]{:S(2)}) copy-start(f32[8,256,256]{2,1,0:T(8,128)S(1)} %fusion.15) | copy-start | bytes 6291460
  162.6 9.8 %collective-permute-start.4 = (f32[1,256,256]{2,1,0:T(8,128)S(1)}, f32[1,256,256]{2,1,0:T(8,128)S(1)}, u32[]{:S(2)}, u32[]{:S(2)}) collective-permute-start(f32[1,256,256]{2,1,0:T(8,128)S(1)} %get-tuple-element.65), channel_id=1, source_target_pairs={{1,0},{2,1},{3,2},{4,3},{5,4},{6,5},{7,6},{8,7},{9,8},{10,9},{11,1... | collective-permute-start | bytes 786440 | tf_op jit(solution)/shard_map/ppermute | solution.py:33
  164.7 7.7 %collective-permute-start.5 = (f32[1,256,256]{2,1,0:T(8,128)S(1)}, f32[1,256,256]{2,1,0:T(8,128)S(1)}, u32[]{:S(2)}, u32[]{:S(2)}) collective-permute-start(f32[1,256,256]{2,1,0:T(8,128)S(1)} %get-tuple-element.66), channel_id=1, source_target_pairs={{0,1},{1,2},{2,3},{3,4},{4,5},{5,6},{6,7},{7,8},{8,9},{9,10},{10,1... | collective-permute-start | bytes 786440 | tf_op jit(solution)/shard_map/ppermute | solution.py:31
  175.5 10.8 %copy-start.9 = (f32[8,256,256]{2,1,0:T(8,128)}, f32[8,256,256]{2,1,0:T(8,128)S(1)}, u32[]{:S(2)}) copy-start(f32[8,256,256]{2,1,0:T(8,128)S(1)} %fusion.23) | copy-start | bytes 6291460
  175.6 10.8 %collective-permute-start.6 = (f32[1,256,256]{2,1,0:T(8,128)S(1)}, f32[1,256,256]{2,1,0:T(8,128)S(1)}, u32[]{:S(2)}, u32[]{:S(2)}) collective-permute-start(f32[1,256,256]{2,1,0:T(8,128)S(1)} %get-tuple-element.63), channel_id=1, source_target_pairs={{1,0},{2,1},{3,2},{4,3},{5,4},{6,5},{7,6},{8,7},{9,8},{10,9},{11,1... | collective-permute-start | bytes 786440 | tf_op jit(solution)/shard_map/ppermute | solution.py:33
  178.1 8.3 %copy-start.21 = (s32[8,256,256]{2,1,0:T(8,128)S(1)}, s32[8,256,256]{2,1,0:T(8,128)}, u32[]{:S(2)}) copy-start(s32[8,256,256]{2,1,0:T(8,128)} %param.12) | copy-start | bytes 6291460
  178.1 8.3 %collective-permute-start.7 = (f32[1,256,256]{2,1,0:T(8,128)S(1)}, f32[1,256,256]{2,1,0:T(8,128)S(1)}, u32[]{:S(2)}, u32[]{:S(2)}) collective-permute-start(f32[1,256,256]{2,1,0:T(8,128)S(1)} %get-tuple-element.64), channel_id=1, source_target_pairs={{0,1},{1,2},{2,3},{3,4},{4,5},{5,6},{6,7},{7,8},{8,9},{9,10},{10,1... | collective-permute-start | bytes 786440 | tf_op jit(solution)/shard_map/ppermute | solution.py:31
  220.3 4.4 copy-start.2
  220.3 4.4 copy-start.10
  224.7 8.3 %copy-start.13 = (f32[8,256,256]{2,1,0:T(8,128)}, f32[8,256,256]{2,1,0:T(8,128)S(1)}, u32[]{:S(2)}) copy-start(f32[8,256,256]{2,1,0:T(8,128)S(1)} %get-tuple-element.31) | copy-start | bytes 6291460
  232.9 7.5 %copy-start.17 = (f32[8,256,256]{2,1,0:T(8,128)}, f32[8,256,256]{2,1,0:T(8,128)S(1)}, u32[]{:S(2)}) copy-start(f32[8,256,256]{2,1,0:T(8,128)S(1)} %get-tuple-element.33) | copy-start | bytes 6291460
  232.9 7.5 %copy-start.18 = (f32[8,256,256]{2,1,0:T(8,128)}, f32[8,256,256]{2,1,0:T(8,128)S(1)}, u32[]{:S(2)}) copy-start(f32[8,256,256]{2,1,0:T(8,128)S(1)} %get-tuple-element.48) | copy-start | bytes 6291460
  233.0 37.0 %collective-permute-start.8 = (f32[1,256,256]{2,1,0:T(8,128)S(1)}, f32[1,256,256]{2,1,0:T(8,128)S(1)}, u32[]{:S(2)}, u32[]{:S(2)}) collective-permute-start(f32[1,256,256]{2,1,0:T(8,128)S(1)} %get-tuple-element.59), channel_id=1, source_target_pairs={{1,0},{2,1},{3,2},{4,3},{5,4},{6,5},{7,6},{8,7},{9,8},{10,9},{11,1... | collective-permute-start | bytes 786440 | tf_op jit(solution)/shard_map/ppermute | solution.py:33
  238.5 31.5 %collective-permute-start.9 = (f32[1,256,256]{2,1,0:T(8,128)S(1)}, f32[1,256,256]{2,1,0:T(8,128)S(1)}, u32[]{:S(2)}, u32[]{:S(2)}) collective-permute-start(f32[1,256,256]{2,1,0:T(8,128)S(1)} %get-tuple-element.60), channel_id=1, source_target_pairs={{0,1},{1,2},{2,3},{3,4},{4,5},{5,6},{6,7},{7,8},{8,9},{9,10},{10,1... | collective-permute-start | bytes 786440 | tf_op jit(solution)/shard_map/ppermute | solution.py:31
  270.0 16.6 %copy-start.3 = (f32[1,8,256,256]{3,2,1,0:T(8,128)S(1)}, f32[1,8,256,256]{3,2,1,0:T(8,128)}, u32[]{:S(2)}) copy-start(f32[1,8,256,256]{3,2,1,0:T(8,128)} %param.9) | copy-start | bytes 6291460
  270.0 16.6 %copy-start.8 = (f32[8,256,256]{2,1,0:T(8,128)S(1)}, f32[8,256,256]{2,1,0:T(8,128)}, u32[]{:S(2)}) copy-start(f32[8,256,256]{2,1,0:T(8,128)} %copy-done.7) | copy-start | bytes 6291460
  286.6 8.3 %copy-start.14 = (f32[8,256,256]{2,1,0:T(8,128)}, f32[8,256,256]{2,1,0:T(8,128)S(1)}, u32[]{:S(2)}) copy-start(f32[8,256,256]{2,1,0:T(8,128)S(1)} %get-tuple-element.21) | copy-start | bytes 6291460
  294.9 12.9 %copy-start.19 = (f32[8,256,256]{2,1,0:T(8,128)}, f32[8,256,256]{2,1,0:T(8,128)S(1)}, u32[]{:S(2)}) copy-start(f32[8,256,256]{2,1,0:T(8,128)S(1)} %get-tuple-element.23) | copy-start | bytes 6291460
  294.9 12.9 %copy-start.20 = (f32[8,256,256]{2,1,0:T(8,128)}, f32[8,256,256]{2,1,0:T(8,128)S(1)}, u32[]{:S(2)}) copy-start(f32[8,256,256]{2,1,0:T(8,128)S(1)} %get-tuple-element.46) | copy-start | bytes 6291460
  295.0 12.8 %collective-permute-start.10 = (f32[1,256,256]{2,1,0:T(8,128)S(1)}, f32[1,256,256]{2,1,0:T(8,128)S(1)}, u32[]{:S(2)}, u32[]{:S(2)}) collective-permute-start(f32[1,256,256]{2,1,0:T(8,128)S(1)} %get-tuple-element.55), channel_id=1, source_target_pairs={{1,0},{2,1},{3,2},{4,3},{5,4},{6,5},{7,6},{8,7},{9,8},{10,9},{11,1... | collective-permute-start | bytes 786440 | tf_op jit(solution)/shard_map/ppermute | solution.py:33
  296.9 10.9 %collective-permute-start.11 = (f32[1,256,256]{2,1,0:T(8,128)S(1)}, f32[1,256,256]{2,1,0:T(8,128)S(1)}, u32[]{:S(2)}, u32[]{:S(2)}) collective-permute-start(f32[1,256,256]{2,1,0:T(8,128)S(1)} %get-tuple-element.56), channel_id=1, source_target_pairs={{0,1},{1,2},{2,3},{3,4},{4,5},{5,6},{6,7},{7,8},{8,9},{9,10},{10,1... | collective-permute-start | bytes 786440 | tf_op jit(solution)/shard_map/ppermute | solution.py:31
  299.3 8.5 %copy-start.5 = (f32[8,256,256]{2,1,0:T(8,128)S(1)}, f32[8,256,256]{2,1,0:T(8,128)}, u32[]{:S(2)}) copy-start(f32[8,256,256]{2,1,0:T(8,128)} %copy-done.4) | copy-start | bytes 6291460
  307.9 16.7 %copy-start.12 = (f32[8,256,256]{2,1,0:T(8,128)S(1)}, f32[8,256,256]{2,1,0:T(8,128)}, u32[]{:S(2)}) copy-start(f32[8,256,256]{2,1,0:T(8,128)} %copy-done.11) | copy-start | bytes 6291460
  334.8 15.3 %copy-start.15 = (f32[8,256,256]{2,1,0:T(8,128)}, f32[8,256,256]{2,1,0:T(8,128)S(1)}, u32[]{:S(2)}) copy-start(f32[8,256,256]{2,1,0:T(8,128)S(1)} %get-tuple-element.13) | copy-start | bytes 6291460
  334.8 15.3 %copy-start.16 = (f32[8,256,256]{2,1,0:T(8,128)}, f32[8,256,256]{2,1,0:T(8,128)S(1)}, u32[]{:S(2)}) copy-start(f32[8,256,256]{2,1,0:T(8,128)S(1)} %get-tuple-element.44) | copy-start | bytes 6291460
  336.2 13.9 %collective-permute-start.12 = (f32[1,256,256]{2,1,0:T(8,128)S(1)}, f32[1,256,256]{2,1,0:T(8,128)S(1)}, u32[]{:S(2)}, u32[]{:S(2)}) collective-permute-start(f32[1,256,256]{2,1,0:T(8,128)S(1)} %get-tuple-element.51), channel_id=1, source_target_pairs={{1,0},{2,1},{3,2},{4,3},{5,4},{6,5},{7,6},{8,7},{9,8},{10,9},{11,1... | collective-permute-start | bytes 786440 | tf_op jit(solution)/shard_map/ppermute | solution.py:33
  339.4 10.7 %collective-permute-start.13 = (f32[1,256,256]{2,1,0:T(8,128)S(1)}, f32[1,256,256]{2,1,0:T(8,128)S(1)}, u32[]{:S(2)}, u32[]{:S(2)}) collective-permute-start(f32[1,256,256]{2,1,0:T(8,128)S(1)} %get-tuple-element.52), channel_id=1, source_target_pairs={{0,1},{1,2},{2,3},{3,4},{4,5},{5,6},{6,7},{7,8},{8,9},{9,10},{10,1... | collective-permute-start | bytes 786440 | tf_op jit(solution)/shard_map/ppermute | solution.py:31
  341.5 8.6 %copy-start.6 = (f32[8,256,256]{2,1,0:T(8,128)S(1)}, f32[8,256,256]{2,1,0:T(8,128)}, u32[]{:S(2)}) copy-start(f32[8,256,256]{2,1,0:T(8,128)} %copy-done.4) | copy-start | bytes 6291460
  442.8 55.4 %copy-start.23 = (f32[1,2,4096]{2,1,0:T(2,128)S(1)}, f32[1,2,4096]{2,1,0:T(2,128)}, u32[]{:S(2)}) copy-start(f32[1,2,4096]{2,1,0:T(2,128)} %copy-done.22) | copy-start | bytes 98308
  442.8 55.4 %copy-start.25 = (f32[2,4096]{1,0:T(2,128)S(1)}, f32[2,4096]{1,0:T(2,128)}, u32[]{:S(2)}) copy-start(f32[2,4096]{1,0:T(2,128)} %copy-done.24) | copy-start | bytes 98308
